TPU v7x, 32 devices: a whole 2x2x4 slice. The times are simulated.
32 devices in a mesh: groups: 2 (over x), ref: 16 (over z, y, core).
Axes of the slice: x: 2, y: 2, z: 4, core: 2. Of those that a mesh axis runs over, the one named last changes fastest.
Arguments:
- long_series: bfloat16 [131072], P(('groups', 'ref')), parts along dimension 0, may hold values from -12 to 12
- queries: bfloat16 [64, 1024], P(('groups', 'ref')), parts along dimension 0, may hold values from -48 to 48
- lengths: int32 [64], P(('groups', 'ref')), parts along dimension 0, may hold values from 512 to 1024, as said below
- groups: int32 [64], P(('groups', 'ref')), parts along dimension 0, may hold values from 0 to 15, as said below
Outputs:
- profile: float32 [64, 1024], P(('groups', 'ref')), parts along dimension 0
There are 2 independent parts, one for each index of `groups`. A program takes and returns all parts, laid end to end along the dimension named above; each array names one. Nothing has to cross between parts.
Inputs may be any that keep to these rules, and one draw needn't show every extreme that they name: `lengths`: multiples of 128. `groups`: region g holds reference blocks g * 1 to (g + 1) * 1 - 1; at most 4 queries name one region, and one region is named by exactly 4.
All inputs are finite; a program needn't handle non-finite values.
Results may differ from a plain program's by a relative error of at most 0.0003.
Values may be sent and summed in bfloat16 or wider, within the bound.
A program may use at most 64 MiB of HBM per device.

v0:
```python
import functools

import jax
import jax.numpy as jnp
from jax import lax
from jax.experimental import pallas as pl
from jax.experimental.pallas import tpu as pltpu
from jax.sharding import PartitionSpec as P

M = 256
LANES = 128
HALVES = M // LANES
SPREAD_FLOOR = 0.25
CHUNK = 4
MASKED = -1e30


def hankel_tiles(rows):
    shape = (LANES, LANES)
    lane = lax.broadcasted_iota(jnp.int32, shape, 1)
    sub = lax.broadcasted_iota(jnp.int32, shape, 0)
    rolled = [
        pltpu.roll(jnp.broadcast_to(row, shape), 1, 1, stride=1, stride_axis=0) for row in rows
    ]
    return [
        jnp.where(lane <= sub, here, there).astype(jnp.bfloat16)
        for here, there in zip(rolled, rolled[1:])
    ]


def toeplitz(row, following):
    shape = (LANES, LANES)
    lane = lax.broadcasted_iota(jnp.int32, shape, 1)
    sub = lax.broadcasted_iota(jnp.int32, shape, 0)
    here = pltpu.roll(jnp.broadcast_to(row, shape), 0, 1, stride=1, stride_axis=0)
    there = pltpu.roll(jnp.broadcast_to(following, shape), 0, 1, stride=1, stride_axis=0)
    return jnp.where(lane >= sub, here, there)


def next_row(x):
    return pltpu.roll(x, x.shape[0] - 1, 0)


def window_stats(x):
    lane = lax.broadcasted_iota(jnp.int32, x.shape, 1)
    total, square = x, jnp.zeros_like(x)
    count = 1
    while count < M:
        def ahead(v):
            if count == LANES:
                return next_row(v)
            rolled = pltpu.roll(v, LANES - count, 1)
            return jnp.where(lane < LANES - count, rolled, next_row(rolled))

        total_ahead, square_ahead = ahead(total), ahead(square)
        gap = total - total_ahead
        square = square + square_ahead + gap * gap * (0.5 / count)
        total = total + total_ahead
        count *= 2
    return total, 1.0 / jnp.sqrt(square * (1.0 / M) + SPREAD_FLOOR)


def join_kernel(members, groups_hbm, lengths_hbm, q_hbm, block_hbm, out_ref,
                series_ref, left_ref, right_ref, mean_ref, total_ref, scale_ref, q_scale_ref, acc_ref, even_ref, odd_ref,
                q_ref, groups_ref, lengths_ref,
                local_sem, send_sem, recv_sem):
    per_device, series_len = q_ref.shape
    q_rows = series_len // LANES
    all_rows = series_ref.shape[0]
    rows = all_rows // members
    full = (series_len - M) // LANES
    tall = full * LANES + 16
    r_pad = rows + 16
    q_pad = q_rows + 8
    me = lax.axis_index("ref")

    def place(d):
        return lax.rem(me + d, members)

    def slot(owner):
        return series_ref.at[pl.ds(pl.multiple_of(owner * rows, rows), rows), :]

    def copy(d, owner):
        return pltpu.make_async_remote_copy(
            src_ref=slot(me), dst_ref=slot(owner), send_sem=send_sem.at[d], recv_sem=recv_sem.at[d],
            device_id={"ref": place(d)}, device_id_type=pl.DeviceIdType.MESH,
        )

    fetches = [
        pltpu.make_async_copy(block_hbm, slot(me), local_sem.at[0]),
        pltpu.make_async_copy(q_hbm, q_ref, local_sem.at[1]),
        pltpu.make_async_copy(groups_hbm, groups_ref, local_sem.at[2]),
        pltpu.make_async_copy(lengths_hbm, lengths_ref, local_sem.at[3]),
    ]
    barrier = pltpu.get_barrier_semaphore()
    for fetch in fetches:
        fetch.start()

    @pl.loop(1, members)
    def _(d):
        pl.semaphore_signal(
            barrier, inc=1, device_id={"ref": place(d)}, device_id_type=pl.DeviceIdType.MESH
        )

    fetches[1].wait()

    flip = (
        lax.broadcasted_iota(jnp.int32, (LANES, LANES), 0)
        + lax.broadcasted_iota(jnp.int32, (LANES, LANES), 1)
        == LANES - 1
    ).astype(jnp.bfloat16)
    q_all = q_ref[...].astype(jnp.float32)
    parts = []
    for p in range(per_device):
        pieces = [q_all[p : p + 1, LANES * a : LANES * (a + 1)] for a in range(q_rows)]
        parts += pieces + [jnp.zeros((q_pad - q_rows, LANES), jnp.float32)]
    q_points = jnp.concatenate(parts, axis=0)
    q_scale_ref[...] = window_stats(q_points)[1]
    q_back = jnp.dot(q_points.astype(jnp.bfloat16), flip, preferred_element_type=jnp.float32)
    for p in range(per_device):
        q_base = p * q_pad
        for a in range(full + HALVES):
            tile = toeplitz(
                q_back[q_base + a : q_base + a + 1], q_back[q_base + a + 1 : q_base + a + 2]
            ).astype(jnp.bfloat16)
            for h in range(HALVES):
                if 0 <= a - h < full:
                    left_ref[p, pl.ds((a - h) * LANES, LANES), pl.ds(h * LANES, LANES)] = tile
                elif a - h == full:
                    left_ref[p, pl.ds(full * LANES, 16), pl.ds(h * LANES, LANES)] = tile[:16]
        mean_ref[p] = jnp.dot(
            left_ref[p], jnp.full((M, LANES), 1.0 / M, jnp.bfloat16), preferred_element_type=jnp.float32
        )

    fetches[0].wait()
    pl.semaphore_wait(barrier, members - 1)

    @pl.loop(1, members)
    def _(d):
        copy(d, me).start()

    fetches[2].wait()
    fetches[3].wait()

    @pl.loop(1, members)
    def _(d):
        copy(d, place(members - d)).wait_recv()

    column = lax.broadcasted_iota(jnp.int32, (r_pad, all_rows), 1)
    wanted = lax.broadcasted_iota(jnp.int32, (r_pad, all_rows), 0)
    picks = [
        jnp.where(column == wanted + groups_ref[p] * rows, 1.0, 0.0).astype(jnp.bfloat16)
        for p in range(per_device)
    ]
    points = jnp.dot(
        jnp.concatenate(picks, axis=0), series_ref[...], preferred_element_type=jnp.float32
    )
    total, scale = window_stats(points)
    total_ref[...] = total
    scale_ref[...] = scale

    for p in range(per_device):
        r_base = p * r_pad
        q_base = p * q_pad
        tiles = hankel_tiles([points[r_base + m : r_base + m + 1] for m in range(rows + HALVES)])
        for m, tile in enumerate(tiles):
            right_ref[m] = tile

        g = groups_ref[p]

        def multiply(products_ref, first):
            right = jnp.concatenate(
                [
                    jnp.concatenate([right_ref[first + h + n] for n in range(CHUNK)], axis=1)
                    for h in range(HALVES)
                ],
                axis=0,
            )
            products_ref[...] = jnp.dot(left_ref[p], right, preferred_element_type=jnp.float32)

        def fold(products_ref, first, last):
            totals = [total_ref[pl.ds(r_base + first + n, 1), :] for n in range(CHUNK)]
            scales = [scale_ref[pl.ds(r_base + first + n, 1), :] for n in range(CHUNK)]
            if last:
                lane = lax.broadcasted_iota(jnp.int32, (1, LANES), 1)
                start = (g * rows + first) * LANES
                limit = all_rows * LANES - M
                floors = [
                    jnp.where(start + n * LANES + lane <= limit, 0.0, MASKED) for n in range(CHUNK)
                ]
            for t in range(0, tall, 16):
                mean = mean_ref[p, pl.ds(t, 16), :]
                best = None
                for n in range(CHUNK):
                    piece = products_ref[pl.ds(t, 16), pl.ds(n * LANES, LANES)]
                    value = (piece - mean * totals[n]) * scales[n]
                    if last:
                        value = value + floors[n]
                    best = value if best is None else jnp.maximum(best, value)
                if not last:
                    best = jnp.maximum(best, acc_ref[pl.ds(t, 16), :])
                acc_ref[pl.ds(t, 16), :] = best

        multiply(even_ref, rows - CHUNK)
        multiply(odd_ref, 0)
        fold(even_ref, rows - CHUNK, True)

        @pl.loop(0, rows // (2 * CHUNK) - 1)
        def _(i):
            first = 2 * CHUNK * i
            multiply(even_ref, first + CHUNK)
            fold(odd_ref, first, False)
            multiply(odd_ref, first + 2 * CHUNK)
            fold(even_ref, first + CHUNK, False)

        fold(odd_ref, rows - 2 * CHUNK, False)

        lane = lax.broadcasted_iota(jnp.int32, (1, LANES), 1)
        limit = lengths_ref[p] - M
        for a in range(q_rows):
            if a < full:
                block = acc_ref[pl.ds(a * LANES, LANES), :]
                best = jnp.max(block.T, axis=0, keepdims=True)
            elif a == full:
                block = acc_ref[pl.ds(a * LANES, 8), :]
                best = jnp.broadcast_to(jnp.max(block, axis=1, keepdims=True)[:1], (1, LANES))
            if a <= full:
                best = best * q_scale_ref[pl.ds(q_base + a, 1), :] * (1.0 / M)
                row = jnp.where(a * LANES + lane <= limit, 2.0 * (1.0 - best), 0.0)
            else:
                row = jnp.zeros((1, LANES), jnp.float32)
            out_ref[pl.ds(p, 1), pl.ds(a * LANES, LANES)] = row

    @pl.loop(1, members)
    def _(d):
        copy(d, me).wait_send()


def join(members, groups, lengths, queries, block):
    per_device, series_len = queries.shape
    rows = block.shape[0]
    tall = (series_len - M) // LANES * LANES + 16
    r_rows = per_device * (rows + 16)
    q_rows = per_device * (series_len // LANES + 8)
    vmem = pl.BlockSpec(memory_space=pltpu.VMEM)
    return pl.pallas_call(
        functools.partial(join_kernel, members),
        out_shape=pltpu.VMEM((per_device, series_len), jnp.float32),
        in_specs=[pl.BlockSpec(memory_space=pl.ANY)] * 4,
        out_specs=vmem,
        scratch_shapes=[
            pltpu.VMEM((members * rows, LANES), jnp.bfloat16),
            pltpu.VMEM((per_device, tall, M), jnp.bfloat16),
            pltpu.VMEM((rows + 1, LANES, LANES), jnp.bfloat16),
            pltpu.VMEM((per_device, tall, LANES), jnp.float32),
            pltpu.VMEM((r_rows, LANES), jnp.float32),
            pltpu.VMEM((r_rows, LANES), jnp.float32),
            pltpu.VMEM((q_rows, LANES), jnp.float32),
            pltpu.VMEM((tall, LANES), jnp.float32),
            pltpu.VMEM((tall, CHUNK * LANES), jnp.float32),
            pltpu.VMEM((tall, CHUNK * LANES), jnp.float32),
            pltpu.VMEM((per_device, series_len), jnp.bfloat16),
            pltpu.SMEM((per_device,), jnp.int32),
            pltpu.SMEM((per_device,), jnp.int32),
            pltpu.SemaphoreType.DMA((4,)),
            pltpu.SemaphoreType.DMA((members,)),
            pltpu.SemaphoreType.DMA((members,)),
        ],
        compiler_params=pltpu.CompilerParams(collective_id=0, has_side_effects=True),
        name="join",
    )(groups, lengths, queries, block)


def body(long_series, queries, lengths, groups):
    members = lax.axis_size("ref")
    return join(members, groups, lengths, queries, long_series.reshape(-1, LANES))


def solution(mesh):
    in_specs = (
        P(("groups", "ref")),
        P(("groups", "ref"), None),
        P(("groups", "ref")),
        P(("groups", "ref")),
    )
    out_specs = P(("groups", "ref"), None)
    return jax.shard_map(body, mesh=mesh, in_specs=in_specs, out_specs=out_specs, check_vma=False)
```

profile of v0, /device:TPU:0, one launch (start us, length us, event | category | flops | bytes accessed | tf_op | source)
XLA Modules:
  0.0 16.9 jit_solution(12539788232753212034)
XLA Ops:
  0.0 16.2 %join.1 = f32[2,1024]{1,0:T(2,128)S(1)} custom-call(s32[2]{0:T(128)} %groups_hbm.1, s32[2]{0:T(128)} %lengths_hbm.1, bf16[2,1024]{1,0:T(2,128)(2,1)} %q_hbm.1, bf16[32,128]{1,0:T(8,128)(2,1)} %bitcast.1), custom_call_target="tpu_custom_call" | custom-call | tf_op jit(solution)/shard_map/join/pallas_call | solution.py:246
  16.3 0.6 %copy.6 = f32[2,1024]{1,0:T(2,128)} copy(f32[2,1024]{1,0:T(2,128)S(1)} %join.1) | data formatting | bytes 16384
where the time goes:
time: 17 us; the launch traced here: 16.9 us
  Pallas kernels  16.2 us (95%)
  local copies, waits for them, and re-layouts  0.6 us (4%)
    pallas_call x1, Pallas kernels, join(): pl.pallas_call(functools.partial(join_kernel, members), out_shape=pltpu.V...  16.2 us
    unnamed x1, local copies, waits for them, and re-layouts  0.6 us

commit v1 on v0

v1 whole, which is shorter than its diff:
```python
import functools

import jax
import jax.numpy as jnp
from jax import lax
from jax.experimental import pallas as pl
from jax.experimental.pallas import tpu as pltpu
from jax.sharding import PartitionSpec as P

M = 256
LANES = 128
WIDE = 2 * LANES
SPREAD_FLOOR = 0.25
CHUNK = 4
PIECE = 16
MASKED = -1e30


def iotas(shape):
    return (
        lax.broadcasted_iota(jnp.int32, shape, 0),
        lax.broadcasted_iota(jnp.int32, shape, 1),
    )


def hankel_tiles(rows):
    shape = (LANES, LANES)
    sub, lane = iotas(shape)
    rolled = [
        pltpu.roll(jnp.broadcast_to(row, shape), 1, 1, stride=1, stride_axis=0) for row in rows
    ]
    return [
        jnp.where(lane <= sub, here, there).astype(jnp.bfloat16)
        for here, there in zip(rolled, rolled[1:])
    ]


def toeplitz(row, following):
    shape = (LANES, LANES)
    sub, lane = iotas(shape)
    here = pltpu.roll(jnp.broadcast_to(row, shape), 0, 1, stride=1, stride_axis=0)
    there = pltpu.roll(jnp.broadcast_to(following, shape), 0, 1, stride=1, stride_axis=0)
    return jnp.where(lane >= sub, here, there)


def next_row(x):
    return pltpu.roll(x, x.shape[0] - 1, 0)


def window_scale(x):
    lane = lax.broadcasted_iota(jnp.int32, x.shape, 1)
    total, square = x, jnp.zeros_like(x)
    count = 1
    while count < M:
        def ahead(v):
            if count == LANES:
                return next_row(v)
            rolled = pltpu.roll(v, LANES - count, 1)
            return jnp.where(lane < LANES - count, rolled, next_row(rolled))

        total_ahead, square_ahead = ahead(total), ahead(square)
        gap = total - total_ahead
        square = square + square_ahead + gap * gap * (0.5 / count)
        total = total + total_ahead
        count *= 2
    return 1.0 / jnp.sqrt(square * (1.0 / M) + SPREAD_FLOOR)


def join_kernel(members, groups_hbm, lengths_hbm, q_hbm, block_hbm, out_ref,
                series_ref, left_ref, mean_ref, points_ref, total_ref, scale_ref,
                q_scale_ref, acc_ref, q_ref, groups_ref, lengths_ref,
                local_sem, send_sem, recv_sem):
    tall = left_ref.shape[1]
    pieces = tall // PIECE
    specs = [pltpu.ACC(x)((PIECE, WIDE), jnp.float32) for x in range(2) for _ in range(pieces)]

    def main(*accs):
        join_body(members, groups_hbm, lengths_hbm, q_hbm, block_hbm, out_ref,
                  series_ref, left_ref, mean_ref, points_ref, total_ref, scale_ref,
                  q_scale_ref, acc_ref, q_ref, groups_ref, lengths_ref,
                  local_sem, send_sem, recv_sem, (accs[:pieces], accs[pieces:]))

    pl.run_scoped(main, *specs)


def join_body(members, groups_hbm, lengths_hbm, q_hbm, block_hbm, out_ref,
              series_ref, left_ref, mean_ref, points_ref, total_ref, scale_ref,
              q_scale_ref, acc_ref, q_ref, groups_ref, lengths_ref,
              local_sem, send_sem, recv_sem, accs):
    per_device, series_len = q_ref.shape
    q_rows = series_len // LANES
    rows = block_hbm.shape[0]
    full = (series_len - M) // LANES
    tall = left_ref.shape[1]
    pieces = tall // PIECE
    q_pad = q_rows + 8
    chunks = rows // CHUNK
    me = lax.axis_index("ref")

    def place(d):
        return lax.rem(me + d, members)

    def slot(owner):
        return series_ref.at[owner]

    def copy(src, d):
        return pltpu.make_async_remote_copy(
            src_ref=src, dst_ref=src, send_sem=send_sem.at[0], recv_sem=recv_sem.at[0],
            device_id={"ref": place(d)}, device_id_type=pl.DeviceIdType.MESH,
        )

    fetches = [
        pltpu.make_async_copy(block_hbm, slot(me), local_sem.at[0]),
        pltpu.make_async_copy(q_hbm, q_ref, local_sem.at[1]),
        pltpu.make_async_copy(groups_hbm, groups_ref, local_sem.at[2]),
        pltpu.make_async_copy(lengths_hbm, lengths_ref, local_sem.at[3]),
    ]
    barrier = pltpu.get_barrier_semaphore()
    for fetch in fetches:
        fetch.start()

    @pl.loop(1, members)
    def _(d):
        pl.semaphore_signal(
            barrier, inc=1, device_id={"ref": place(d)}, device_id_type=pl.DeviceIdType.MESH
        )

    series_ref[members] = jnp.zeros((rows, LANES), jnp.bfloat16)
    acc_ref[...] = jnp.full(acc_ref.shape, MASKED, jnp.float32)
    fetches[0].wait()
    pl.semaphore_wait(barrier, members - 1)

    @pl.loop(1, members)
    def _(d):
        copy(slot(me), d).start()

    fetches[1].wait()
    fetches[2].wait()
    fetches[3].wait()

    sub, lane = iotas((WIDE, WIDE))
    flip = jnp.where(sub + lane == LANES - 1, 1.0, 0.0).astype(jnp.bfloat16)
    ones = jnp.full((WIDE, WIDE), 1.0 / M, jnp.bfloat16)
    q_all = q_ref[...].astype(jnp.float32)
    parts = []
    for p in range(per_device):
        row_list = [q_all[p : p + 1, LANES * a : LANES * (a + 1)] for a in range(q_rows)]
        parts += row_list + [jnp.zeros((q_pad - q_rows, LANES), jnp.float32)]
    q_points = jnp.concatenate(parts, axis=0)
    q_scale_ref[...] = window_scale(q_points)
    q_lhs = jnp.concatenate([q_points, jnp.zeros_like(q_points)], axis=1).astype(jnp.bfloat16)
    pltpu.matmul_push_rhs(flip, 0, 0)
    for p in range(per_device):
        pltpu.matmul_acc_lhs(
            accs[0][p], q_lhs[p * q_pad : (p + 1) * q_pad], load_staged_rhs=None if p else 0
        )
    for x in range(2):
        pltpu.matmul_push_rhs(ones, 0, x)
    for p in range(per_device):
        q_back = pltpu.matmul_pop(accs[0][p])[:, :LANES]
        for a in range(full + 2):
            tile = toeplitz(q_back[a : a + 1], q_back[a + 1 : a + 2]).astype(jnp.bfloat16)
            for h in range(2):
                if 0 <= a - h < full:
                    left_ref[p, pl.ds((a - h) * LANES, LANES), pl.ds(h * LANES, LANES)] = tile
                elif a - h == full:
                    left_ref[p, pl.ds(full * LANES, PIECE), pl.ds(h * LANES, LANES)] = tile[:PIECE]
    for p in range(per_device):
        for i in range(pieces):
            x = i % 2
            pltpu.matmul_acc_lhs(
                accs[x][i], left_ref[p, pl.ds(i * PIECE, PIECE), :],
                load_staged_rhs=0 if p == 0 and i < 2 else None,
            )
        for i in range(pieces):
            mean_ref[p, pl.ds(i * PIECE, PIECE), :] = pltpu.matmul_pop(accs[i % 2][i])[:, :LANES]

    near = jnp.where((lane >= LANES) | (sub >= LANES) | (sub >= lane), 1.0, 0.0).astype(jnp.bfloat16)
    far = jnp.where((sub < LANES) & (sub < lane), 1.0, 0.0).astype(jnp.bfloat16)
    for x in range(2):
        pltpu.matmul_push_rhs(near, 0, x)
        pltpu.matmul_push_rhs(far, 1, x)

    whole = series_ref.at[pl.ds(0, members - 1)]
    copy(whole, 1).wait_recv()

    for p in range(per_device):
        g = groups_ref[p]
        block = series_ref[g].astype(jnp.float32)
        ahead = series_ref[g + 1].astype(jnp.float32)
        points_ref[p, pl.ds(0, rows), :] = block
        points_ref[p, pl.ds(rows, 8), :] = ahead[:8]
        shape = (8, LANES)
        spot = lax.broadcasted_iota(jnp.int32, shape, 1)
        tail = jnp.concatenate([block[rows - 2 :], ahead[:6]], axis=0)
        moved = pltpu.roll(block[rows - 8 :], LANES - 1, 1)
        moved = jnp.where(spot < LANES - 1, moved, next_row(moved))
        moved = jnp.concatenate([moved[4:], moved[:4]], axis=0)
        final = jnp.full(shape, g, jnp.int32) == members - 1
        points_ref[p, pl.ds(rows + 8, 8), :] = jnp.where(final, moved, tail)
    for p in range(per_device):
        x = p % 2
        here, ahead, beyond = (points_ref[p, pl.ds(s, rows + PIECE), :] for s in range(3))

        def operand(f):
            close = jnp.concatenate([f(here), f(ahead)], axis=1)
            away = jnp.concatenate([f(beyond), jnp.zeros_like(f(beyond))], axis=1)
            return close, away

        def high(v):
            return (v * v).astype(jnp.bfloat16)

        def low(v):
            return (v * v - high(v).astype(jnp.float32)).astype(jnp.bfloat16)

        plain = operand(lambda v: v.astype(jnp.bfloat16))
        squares = [operand(high), operand(low)]
        stat_pieces = rows // PIECE + 1
        for s in range(2):
            for t in range(stat_pieces):
                cut = slice(t * PIECE, (t + 1) * PIECE)
                pltpu.matmul_acc_lhs(
                    accs[x][2 * t], plain[s][cut], load_staged_rhs=s if t == 0 else None
                )
                for square in squares:
                    pltpu.matmul_acc_lhs(accs[x][2 * t + 1], square[s][cut])
        for t in range(stat_pieces):
            total = pltpu.matmul_pop(accs[x][2 * t])[:, :LANES]
            square = pltpu.matmul_pop(accs[x][2 * t + 1])[:, :LANES]
            mean = total * (1.0 / M)
            spread = jnp.maximum(square * (1.0 / M) - mean * mean, 0.0)
            total_ref[p, pl.ds(t * PIECE, PIECE), :] = total
            scale_ref[p, pl.ds(t * PIECE, PIECE), :] = 1.0 / jnp.sqrt(spread + SPREAD_FLOOR)

    half = rows // 2

    def starts(c):
        return 2 * c, jnp.where(c == chunks - 1, rows + 8, half + 2 * c)

    def push(k):
        p, c = k // chunks, k % chunks
        for x, first in enumerate(starts(c)):
            tiles = hankel_tiles([points_ref[p, pl.ds(first + m, 1), :] for m in range(4)])
            rhs = jnp.concatenate(
                [
                    jnp.concatenate([tiles[0], tiles[1]], axis=1),
                    jnp.concatenate([tiles[1], tiles[2]], axis=1),
                ],
                axis=0,
            )
            pltpu.matmul_push_rhs(rhs, 0, x)

    third = -(-pieces // 3)
    parts = [range(s, min(s + third, pieces)) for s in range(0, pieces, third)]

    def multiply(k, part):
        for i in parts[part]:
            lhs = left_ref[k // chunks, pl.ds(i * PIECE, PIECE), :]
            for x in range(2):
                pltpu.matmul_acc_lhs(accs[x][i], lhs, load_staged_rhs=None if i else 0)

    def fold(k, part):
        p, c = k // chunks, k % chunks
        at_rows = [first + n for first in starts(c) for n in range(2)]
        totals = [total_ref[p, pl.ds(at, 1), :] for at in at_rows]
        scales = [scale_ref[p, pl.ds(at, 1), :] for at in at_rows]
        for i in parts[part]:
            at = pl.ds(i * PIECE, PIECE)
            mean = mean_ref[p, at, :]
            popped = [pltpu.matmul_pop(accs[x][i]) for x in range(2)]
            best = acc_ref[p, at, :]
            for n in range(CHUNK):
                piece = popped[n // 2][:, (n % 2) * LANES : (n % 2 + 1) * LANES]
                best = jnp.maximum(best, (piece - mean * totals[n]) * scales[n])
            acc_ref[p, at, :] = best

    def finish(p):
        spot = lax.broadcasted_iota(jnp.int32, (1, LANES), 1)
        limit = lengths_ref[p] - M
        for a in range(q_rows):
            if a < full:
                block = acc_ref[p, pl.ds(a * LANES, LANES), :]
                best = jnp.max(block.T, axis=0, keepdims=True)
            elif a == full:
                block = acc_ref[p, pl.ds(a * LANES, 8), :]
                best = jnp.broadcast_to(jnp.max(block, axis=1, keepdims=True)[:1], (1, LANES))
            if a <= full:
                best = best * q_scale_ref[pl.ds(p * q_pad + a, 1), :] * (1.0 / M)
                row = jnp.where(a * LANES + spot <= limit, 2.0 * (1.0 - best), 0.0)
            else:
                row = jnp.zeros((1, LANES), jnp.float32)
            out_ref[pl.ds(p, 1), pl.ds(a * LANES, LANES)] = row

    steps = per_device * chunks
    push(0)
    multiply(0, 0)
    multiply(0, 1)
    multiply(0, 2)
    push(1)
    fold(0, 0)

    @pl.loop(1, steps)
    def _(k):
        multiply(k, 0)
        fold(k - 1, 1)
        multiply(k, 1)
        fold(k - 1, 2)
        multiply(k, 2)
        push(lax.rem(k + 1, steps))
        fold(k, 0)

    fold(steps - 1, 1)
    fold(steps - 1, 2)
    for x in range(2):
        pltpu.matmul_acc_lhs(accs[x][0], left_ref[0, pl.ds(0, PIECE), :], load_staged_rhs=0)
        pltpu.matmul_pop(accs[x][0])
    for p in range(per_device):
        finish(p)
    copy(whole, 1).wait_send()


def join(members, groups, lengths, queries, block):
    per_device, series_len = queries.shape
    rows = block.shape[0]
    tall = (series_len - M) // LANES * LANES + PIECE
    q_rows = per_device * (series_len // LANES + 8)
    vmem = pl.BlockSpec(memory_space=pltpu.VMEM)
    return pl.pallas_call(
        functools.partial(join_kernel, members),
        out_shape=pltpu.VMEM((per_device, series_len), jnp.float32),
        in_specs=[pl.BlockSpec(memory_space=pl.ANY)] * 4,
        out_specs=vmem,
        scratch_shapes=[
            pltpu.VMEM((members + 1, rows, LANES), jnp.bfloat16),
            pltpu.VMEM((per_device, tall, M), jnp.bfloat16),
            pltpu.VMEM((per_device, tall, LANES), jnp.float32),
            pltpu.VMEM((per_device, rows + 24, LANES), jnp.float32),
            pltpu.VMEM((per_device, rows + PIECE, LANES), jnp.float32),
            pltpu.VMEM((per_device, rows + PIECE, LANES), jnp.float32),
            pltpu.VMEM((q_rows, LANES), jnp.float32),
            pltpu.VMEM((per_device, tall, LANES), jnp.float32),
            pltpu.VMEM((per_device, series_len), jnp.bfloat16),
            pltpu.SMEM((per_device,), jnp.int32),
            pltpu.SMEM((per_device,), jnp.int32),
            pltpu.SemaphoreType.DMA((4,)),
            pltpu.SemaphoreType.DMA((1,)),
            pltpu.SemaphoreType.DMA((1,)),
        ],
        compiler_params=pltpu.CompilerParams(collective_id=0, has_side_effects=True),
        name="join",
    )(groups, lengths, queries, block)


def body(long_series, queries, lengths, groups):
    members = lax.axis_size("ref")
    return join(members, groups, lengths, queries, long_series.reshape(-1, LANES))


def solution(mesh):
    in_specs = (
        P(("groups", "ref")),
        P(("groups", "ref"), None),
        P(("groups", "ref")),
        P(("groups", "ref")),
    )
    out_specs = P(("groups", "ref"), None)
    return jax.shard_map(body, mesh=mesh, in_specs=in_specs, out_specs=out_specs, check_vma=False)
```

time: 17 us -> 16.5 us (0.971)
  Pallas kernels: 16.2 us -> 15.7 us
    pallas_call x1, Pallas kernels: 16.2 us -> 15.7 us  [join(): pl.pallas_call(functools.partial(join_kernel, members), out_shape=pltpu.V...]
where the time goes in v1:
time: 16.5 us; the launch traced here: 16.3 us
  Pallas kernels  15.7 us (95%)
  local copies, waits for them, and re-layouts  0.6 us (4%)
    pallas_call x1, Pallas kernels, join(): pl.pallas_call(functools.partial(join_kernel, members), out_shape=pltpu.V...  15.7 us
    unnamed x1, local copies, waits for them, and re-layouts  0.6 us

profile of v1, /device:TPU:0, one launch (start us, length us, event | category | flops | bytes accessed | tf_op | source)
XLA Modules:
  0.0 16.3 jit_solution(7671363781858132879)
XLA Ops:
  0.0 15.7 %join.1 = f32[2,1024]{1,0:T(2,128)S(1)} custom-call(s32[2]{0:T(128)} %groups_hbm.1, s32[2]{0:T(128)} %lengths_hbm.1, bf16[2,1024]{1,0:T(2,128)(2,1)} %q_hbm.1, bf16[32,128]{1,0:T(8,128)(2,1)} %bitcast.1), custom_call_target="tpu_custom_call" | custom-call | tf_op jit(solution)/shard_map/join/pallas_call | solution.py:328
  15.7 0.6 %copy.6 = f32[2,1024]{1,0:T(2,128)} copy(f32[2,1024]{1,0:T(2,128)S(1)} %join.1) | data formatting | bytes 16384
